TPU v7x, 32 devices: a whole 2x2x4 slice. The times are simulated.
32 devices in a mesh: row: 8 (over z, y), col: 4 (over x, core).
Axes of the slice: x: 2, y: 2, z: 4, core: 2. Of those that a mesh axis runs over, the one named last changes fastest.
Arguments:
- layer_input: bfloat16 [2048, 8192], P('row'), may hold values from -7 to 7
- gain: float32 [8192], replicated, may hold values from 0.5 to 6
- d_query: bfloat16 [2048, 4096], P('row', 'col'), may hold values from -6 to 6
- d_keyval: bfloat16 [2048, 2048], P('row', 'col'), may hold values from -6 to 6
- w_query: bfloat16 [8192, 4096], P('row', 'col'), may hold values from -0.0625 to 0.0625
- w_keyval: bfloat16 [8192, 2048], P('row', 'col'), may hold values from -1 to 1
- d_resid: bfloat16 [2048, 8192], P('row', 'col'), may hold values from -6 to 6
Outputs:
- d_input: bfloat16 [2048, 8192], P('row', 'col')
- grad_wq: bfloat16 [8192, 4096], P('row', 'col')
- grad_wkv: bfloat16 [8192, 2048], P('row', 'col')
- grad_gain: float32 [8192], P('col')
- grad_square_sum: float32 [], replicated
All inputs are finite; a program needn't handle non-finite values.
Results may differ from a plain program's by a relative error of at most 0.023.
Values may be sent and summed in bfloat16 or wider, within the bound.
A program may use at most 128 MiB of HBM per device.

v0:
```python
import math
import jax
import jax.numpy as jnp
from jax import lax
from jax.sharding import PartitionSpec as P

epsilon = 1e-05


def local(layer_input, gain, d_query, d_keyval, w_query, w_keyval, d_resid):
    inputs = layer_input.astype(jnp.float32)
    inv_rms = lax.rsqrt(jnp.mean(inputs * inputs, axis=1, keepdims=True) + epsilon)
    normed = (inputs * inv_rms * gain).astype(jnp.bfloat16)
    model_width = inputs.shape[1]
    local_tokens = inputs.shape[0]
    tokens_all = local_tokens * lax.axis_size("row")
    scaling = 1.0 / math.sqrt(tokens_all)
    weight_scale = 1.0 / math.sqrt(local_tokens)
    contract_cols = (((1,), (1,)), ((), ()))
    query_cols = d_query.shape[1]
    cotangent = jnp.concatenate([d_query, d_keyval], axis=1)
    all_cotangents = lax.all_gather(cotangent, "row", axis=0, tiled=True)
    weights = jnp.concatenate([w_query, w_keyval], axis=1)
    partial_value = lax.dot_general(
        all_cotangents, weights, contract_cols, preferred_element_type=jnp.float32
    )
    reduced = lax.psum_scatter(
        partial_value.astype(jnp.bfloat16), "col", scatter_dimension=0, tiled=True
    )
    n_row, n_col = (lax.axis_size("row"), lax.axis_size("col"))
    fold = n_row // n_col
    pieces = reduced.reshape(fold, local_tokens, reduced.shape[1])
    row, col = (lax.axis_index("row"), lax.axis_index("col"))
    arrived = []
    for shift in range(fold):
        pairs = [
            (r * n_col + c, (fold * c + (r + shift) % fold) * n_col + r // fold)
            for r in range(n_row)
            for c in range(n_col)
        ]
        piece = lax.dynamic_index_in_dim(pieces, (row + shift) % fold, 0, keepdims=False)
        arrived.append(lax.ppermute(piece, ("row", "col"), pairs))
    arrived = jnp.stack(arrived)
    feature_grad = jnp.concatenate(
        [
            lax.dynamic_index_in_dim(arrived, (row - j + fold) % fold, 0, keepdims=False)
            for j in range(fold)
        ],
        axis=1,
    ).astype(jnp.float32)
    slice_width = feature_grad.shape[1]
    col_start = lax.axis_index("col") * slice_width
    input_part = lax.dynamic_slice_in_dim(inputs, col_start, slice_width, 1)
    gain_part = lax.dynamic_slice_in_dim(gain, col_start, slice_width, 0)
    weighted = gain_part * feature_grad
    token_dot = lax.psum(jnp.sum(weighted * input_part, axis=1, keepdims=True), "col")
    d_input = (
        d_resid.astype(jnp.float32)
        + inv_rms * weighted
        - input_part * inv_rms**3 * token_dot / model_width
    ).astype(jnp.bfloat16)
    gain_partial = jnp.sum(feature_grad * input_part * inv_rms, axis=0) * scaling
    cotangent = jnp.concatenate([d_query, d_keyval], axis=1)
    columns = lax.all_to_all(normed, "row", split_axis=1, concat_axis=0, tiled=True)
    groups = lax.axis_size("row")
    column_blocks = columns.reshape(groups, local_tokens, columns.shape[1])
    grad_blocks = all_cotangents.reshape(groups, local_tokens, all_cotangents.shape[1])
    blocks = (
        lax.dot_general(
            column_blocks,
            grad_blocks,
            (((1,), (1,)), ((0,), (0,))),
            preferred_element_type=jnp.float32,
        )
        * weight_scale
    )
    summed = jnp.sum(blocks.astype(jnp.bfloat16).astype(jnp.float32), axis=0)
    grad_wq = summed[:, :query_cols].astype(jnp.bfloat16)
    grad_wkv = summed[:, query_cols:].astype(jnp.bfloat16)
    query_f = grad_wq.astype(jnp.float32)
    keyval_f = grad_wkv.astype(jnp.float32)
    tile_square = jnp.sum(query_f * query_f) + jnp.sum(keyval_f * keyval_f)
    grad_gain = lax.psum(gain_partial, "row")
    leading = jnp.where(
        lax.axis_index("row") == 0, jnp.sum(grad_gain * grad_gain), jnp.float32(0.0)
    )
    grand_total = lax.psum(tile_square + leading, ("row", "col"))
    grad_square_sum = grand_total / jnp.float32(model_width)
    return (d_input, grad_wq, grad_wkv, grad_gain, grad_square_sum)


def solution(mesh):
    placed = (
        P("row", None),
        P(),
        P("row", "col"),
        P("row", "col"),
        P("row", "col"),
        P("row", "col"),
        P("row", "col"),
    )
    return jax.shard_map(
        local,
        mesh=mesh,
        in_specs=placed,
        out_specs=(P("row", "col"), P("row", "col"), P("row", "col"), P("col"), P()),
        check_vma=False,
    )
```

profile of v0, /device:TPU:13, one launch (start us, length us, event | category | flops | bytes accessed | tf_op | source)
XLA Modules:
  0.0 376.0 jit_solution(1316032979656445743)
XLA Ops:
  7.2 0.0 copy-start.2
  7.2 0.0 all-gather.2.cloned.1.call-start
  7.2 2.1 pad_maximum_fusion.1
  9.3 0.0 all-gather.2.cloned.1.call-update
  9.3 0.0 copy-start
  9.3 3.3 multiply_reduce_fusion
  12.6 0.2 copy-done
  12.8 3.1 multiply_convert_fusion.1
  15.9 6.5 %copy.12 = bf16[256,8192]{0,1:T(8,128)(2,1)} copy(bf16[256,8192]{1,0:T(8,128)(2,1)} %multiply_convert_fusion.1) | data formatting | bytes 8388608 | tf_op jit(solution)/shard_map/convert_element_type | solution.py:13
  22.3 5.8 %all-to-all-start = ((bf16[256,8,1024]{0,2,1:T(8,128)(2,1)}), bf16[256,8,1024]{0,2,1:T(8,128)(2,1)}, u32[]{:S(2)}, u32[]{:S(2)}) async-start(bf16[256,8,1024]{0,2,1:T(8,128)(2,1)} %bitcast.18), calls=%async_computation.1 | async-start | bytes 8388608 | tf_op jit(solution)/shard_map/all_to_all | solution.py:64
  28.1 150.8 %all-gather.2.cloned.1.call-done = bf16[2048,1536]{1,0:T(8,128)(2,1)} async-done(((bf16[256,1536]{1,0:T(8,128)(2,1)}), bf16[2048,1536]{1,0:T(8,128)(2,1)}) %all-gather.2.cloned.1.call-update) | async-done | bytes 6291472 | tf_op jit(solution)/shard_map/all_gather | solution.py:22
  179.0 10.4 %convolution_convert_fusion = bf16[2048,1024]{1,0:T(8,128)(2,1)} fusion(bf16[2048,1536]{1,0:T(8,128)(2,1)} %all-gather.2.cloned.1.call-done, bf16[1024,512]{1,0:T(8,128)(2,1)} %param.12, bf16[1024,1024]{1,0:T(8,128)(2,1)S(1)} %copy-done.4), kind=kOutput, calls=%fused_computation.6 | convolution fusion | flops 6450839552 | bytes 13631488 | tf_op jit(solution)/shard_map/dot_general | solution.py:24
  189.4 0.0 reduce-scatter.2.cloned.1.call-update
  189.5 6.4 %convert_element_type.33 = f32[256,8192]{1,0:T(8,128)} convert(bf16[256,8192]{1,0:T(8,128)(2,1)} %param.7) | non-fusion elementwise | flops 2097152 | bytes 12582912 | tf_op jit(solution)/shard_map/convert_element_type | solution.py:11
  195.9 0.0 all-to-all-done
  195.9 10.9 %fusion = bf16[1024,1536]{1,0:T(8,128)(2,1)S(1)} fusion(bf16[8,256,1536]{2,1,0:T(8,128)(2,1)} %bitcast.20, bf16[256,8,1024]{0,2,1:T(8,128)(2,1)} %all-to-all-done), kind=kOutput, calls=%fused_computation.3 | convolution fusion | flops 6478626816 | bytes 13631488 | tf_op jit(solution)/shard_map/dot_general | solution.py:69
  206.8 36.0 %reduce-scatter.2.cloned.1.call-done = bf16[512,1024]{1,0:T(8,128)(2,1)} async-done(((bf16[2048,1024]{1,0:T(8,128)(2,1)}), bf16[512,1024]{1,0:T(8,128)(2,1)}) %reduce-scatter.2.cloned.1.call-update) | async-done | bytes 1048592 | tf_op jit(solution)/shard_map/reduce_scatter | solution.py:27
  242.8 2.3 dynamic-slice_bitcast_fusion
  245.1 0.3 collective-permute-start.1
  245.3 5.3 %collective-permute-start = (bf16[256,1024]{1,0:T(8,128)(2,1)}, bf16[256,1024]{1,0:T(8,128)(2,1)}, u32[]{:S(2)}, u32[]{:S(2)}) collective-permute-start(bf16[256,1024]{1,0:T(8,128)(2,1)} %get-tuple-element.14), channel_id=1, source_target_pairs={{0,0},{1,8},{2,16},{3,24},{4,4},{5,12},{6,20},{7,28},{8,1},{9,9},{... | collective-permute-start | bytes 1572872 | tf_op jit(solution)/shard_map/ppermute | solution.py:42
  250.7 2.0 multiply_reduce_fusion.2
  252.7 2.9 multiply_reduce_fusion.1
  257.1 2.3 collective-permute-done.1
  259.3 0.0 collective-permute-done
  259.3 1.6 fusion.16
  260.9 2.2 fusion.12
  263.2 47.4 %psum.22 = f32[2048]{0:T(1024)S(1)} all-reduce(f32[2048]{0:T(1024)S(1)} %broadcast_multiply_fusion), channel_id=1, replica_groups=mesh['row'=8,'col'=4] {'row'}, use_global_device_ids=true, to_apply=%region_6.7 | all-reduce | flops 2048 | bytes 16384 | tf_op jit(solution)/shard_map/psum | solution.py:83
  310.5 0.0 copy-start.3
  310.5 0.6 multiply_reduce_fusion.3
  311.8 45.0 %psum.23 = f32[]{:T(128)} all-reduce(f32[]{:T(128)S(6)} %add.80), channel_id=1, replica_groups=mesh['row'=8,'col'=4] {'row','col'}, use_global_device_ids=true, to_apply=%region_10.11 | all-reduce | flops 1 | bytes 8 | tf_op jit(solution)/shard_map/psum | solution.py:87
  356.8 7.3 %psum.21 = f32[256]{0:T(256)S(1)} all-reduce(f32[256]{0:T(256)S(1)} %get-tuple-element.6), channel_id=1, replica_groups=mesh['row'=8,'col'=4] {'col'}, use_global_device_ids=true, to_apply=%region_3.4 | all-reduce | flops 256 | bytes 2048 | tf_op jit(solution)/shard_map/psum | solution.py:56
  364.8 3.3 fusion.9
  (10 shorter events, 0.0 us)
Async XLA Ops:
  7.2 5.4 %copy-start.2 = (f32[8192]{0:T(1024)S(1)}, f32[8192]{0:T(1024)}, u32[]{:S(2)}) copy-start(f32[8192]{0:T(1024)} %param.8) | copy-start | bytes 98308
  7.2 171.8 %all-gather.2.cloned.1.call-start = ((), (), s32[]{:S(2)}) async-start(), calls=%async_computation.2 | async-start | bytes 7077888 | tf_op jit(solution)/shard_map/all_gather | solution.py:22
  9.3 3.5 copy-start
  22.3 156.6 %copy-start.4 = (bf16[1024,1024]{1,0:T(8,128)(2,1)S(1)}, bf16[1024,1024]{1,0:T(8,128)(2,1)}, u32[]{:S(2)}) copy-start(bf16[1024,1024]{1,0:T(8,128)(2,1)} %param.11) | copy-start | bytes 6291460
  22.3 173.5 %all-to-all-start = ((bf16[256,8,1024]{0,2,1:T(8,128)(2,1)}), bf16[256,8,1024]{0,2,1:T(8,128)(2,1)}, u32[]{:S(2)}, u32[]{:S(2)}) async-start(bf16[256,8,1024]{0,2,1:T(8,128)(2,1)} %bitcast.18), calls=%async_computation.1 | async-start | bytes 8388608 | tf_op jit(solution)/shard_map/all_to_all | solution.py:64
  28.1 214.7 %reduce-scatter.2.cloned.1.call-start = ((), (), s32[]{:S(2)}) async-start(), calls=%async_computation.3 | async-start | bytes 5242880 | tf_op jit(solution)/shard_map/reduce_scatter | solution.py:27
  245.1 14.3 %collective-permute-start.1 = (bf16[256,1024]{1,0:T(8,128)(2,1)}, bf16[256,1024]{1,0:T(8,128)(2,1)}, u32[]{:S(2)}, u32[]{:S(2)}) collective-permute-start(bf16[256,1024]{1,0:T(8,128)(2,1)} %get-tuple-element.13), channel_id=1, source_target_pairs={{0,4},{1,12},{2,20},{3,28},{4,0},{5,8},{6,16},{7,24},{8,5},{9,13},... | collective-permute-start | bytes 1572872 | tf_op jit(solution)/shard_map/ppermute | solution.py:42
  245.3 14.0 %collective-permute-start = (bf16[256,1024]{1,0:T(8,128)(2,1)}, bf16[256,1024]{1,0:T(8,128)(2,1)}, u32[]{:S(2)}, u32[]{:S(2)}) collective-permute-start(bf16[256,1024]{1,0:T(8,128)(2,1)} %get-tuple-element.14), channel_id=1, source_target_pairs={{0,0},{1,8},{2,16},{3,24},{4,4},{5,12},{6,20},{7,28},{8,1},{9,9},{... | collective-permute-start | bytes 1572872 | tf_op jit(solution)/shard_map/ppermute | solution.py:42
  255.7 109.1 %copy-start.1 = (bf16[256,2048]{1,0:T(8,128)(2,1)S(1)}, bf16[256,2048]{1,0:T(8,128)(2,1)}, u32[]{:S(2)}) copy-start(bf16[256,2048]{1,0:T(8,128)(2,1)} %param.13) | copy-start | bytes 3145732
  310.5 57.5 %copy-start.3 = (f32[2048]{0:T(1024)}, f32[2048]{0:T(1024)S(1)}, u32[]{:S(2)}) copy-start(f32[2048]{0:T(1024)S(1)} %psum.22) | copy-start | bytes 24580
Sparse Core Ops, SparseCore 0:
  10.7 168.1 all-gather.1
  189.5 53.2 reduce-scatter.1
where the time goes:
time: 377 us; the launch traced here: 376 us
  waiting for transfers between devices  189 us (50%)
  blocking collectives  99.7 us (26%)
  other arithmetic  27.5 us (7%)
  matrix products  21.3 us (6%)
  between operations  18 us (5%)
  starting transfers between devices  11.4 us (3%)
  local copies, waits for them, and re-layouts  8.96 us (2%)
    all_gather x1, waiting for transfers between devices, local(): all_cotangents = lax.all_gather(cotangent, 'row', axis=0, tiled=True)  151 us
    psum x1, blocking collectives, local(): grad_gain = lax.psum(gain_partial, 'row')  47.4 us
    psum x1, blocking collectives, local(): grand_total = lax.psum(tile_square + leading, ('row', 'col'))  45 us
    reduce_scatter x1, waiting for transfers between devices, local(): lax.psum_scatter(partial_value.astype(jnp.bfloat16), 'col', scatter_dimen...  36 us
    dot_general x1, matrix products, local(): lax.dot_general(column_blocks, grad_blocks, (((1,), (1,)), ((0,), (0,))),...  10.9 us
    dot_general x1, matrix products, local(): lax.dot_general(all_cotangents, weights, contract_cols, preferred_element...  10.4 us
  transfers between devices with their start and end apart: 5, of which 3 were waited for; matrix products, arithmetic and copies ran while one was open for 12% of the time, Pallas kernels for 0%

commit v1 on v0

--- a/solution.py
+++ b/solution.py
@@ -80,7 +80,11 @@
     query_f = grad_wq.astype(jnp.float32)
     keyval_f = grad_wkv.astype(jnp.float32)
     tile_square = jnp.sum(query_f * query_f) + jnp.sum(keyval_f * keyval_f)
-    grad_gain = lax.psum(gain_partial, "row")
+    grad_gain = gain_partial
+    for hop in (1, 2, 4):
+        grad_gain = grad_gain + lax.ppermute(
+            grad_gain, "row", [(dev, dev ^ hop) for dev in range(8)]
+        )
     leading = jnp.where(
         lax.axis_index("row") == 0, jnp.sum(grad_gain * grad_gain), jnp.float32(0.0)
     )

time: 377 us -> 365 us (0.968)
  blocking collectives: 99.7 us -> 45.1 us
  starting transfers between devices: 11.4 us -> 55.7 us
  waiting for transfers between devices: 189 us -> 182 us
    all_gather x1, waiting for transfers between devices: 151 us -> 97.9 us  [local(): all_cotangents = lax.all_gather(cotangent, 'row', axis=0, tiled=True)]
    all_to_all x1, waiting for transfers between devices: 0.01 us -> 51.9 us  [local(): lax.all_to_all(normed, 'row', split_axis=1, concat_axis=0, tiled=True)]
    ppermute x0 -> x3, starting transfers between devices: none -> 47.8 us  [local(): lax.ppermute(grad_gain, 'row', [(dev, dev ^ hop) for dev in range(8)])]
    psum x1 -> x0, blocking collectives: 47.4 us -> none  [local(): grad_gain = lax.psum(gain_partial, 'row')]
    reduce_scatter x1, waiting for transfers between devices: 36 us -> 26.1 us  [local(): lax.psum_scatter(partial_value.astype(jnp.bfloat16), 'col', scatter_dimen...]
    psum x1, blocking collectives: 45 us -> 40 us  [local(): grand_total = lax.psum(tile_square + leading, ('row', 'col'))]
    ppermute x2, starting transfers between devices: 5.61 us -> 1.21 us  [local(): arrived.append(lax.ppermute(piece, ('row', 'col'), pairs))]
  transfers between devices with their start and end apart: 5 -> 8, of which waited for: 3 -> 4; matrix products, arithmetic and copies ran while one was open for 12% -> 12% of each run, Pallas kernels for 0% -> 0%
where the time goes in v1:
time: 365 us; the launch traced here: 362 us
  waiting for transfers between devices  182 us (50%)
  starting transfers between devices  55.7 us (15%)
  blocking collectives  45.1 us (12%)
  other arithmetic  30 us (8%)
  matrix products  23.8 us (7%)
  between operations  17.9 us (5%)
  local copies, waits for them, and re-layouts  8.13 us (2%)
    all_gather x1, waiting for transfers between devices, local(): all_cotangents = lax.all_gather(cotangent, 'row', axis=0, tiled=True)  97.9 us
    all_to_all x1, waiting for transfers between devices, local(): lax.all_to_all(normed, 'row', split_axis=1, concat_axis=0, tiled=True)  51.9 us
    ppermute x3, starting transfers between devices, local(): lax.ppermute(grad_gain, 'row', [(dev, dev ^ hop) for dev in range(8)])  47.8 us
    psum x1, blocking collectives, local(): grand_total = lax.psum(tile_square + leading, ('row', 'col'))  40 us
    reduce_scatter x1, waiting for transfers between devices, local(): lax.psum_scatter(partial_value.astype(jnp.bfloat16), 'col', scatter_dimen...  26.1 us
    dot_general x1, matrix products, local(): lax.dot_general(column_blocks, grad_blocks, (((1,), (1,)), ((0,), (0,))),...  12.6 us
    dot_general x1, matrix products, local(): lax.dot_general(all_cotangents, weights, contract_cols, preferred_element...  11.1 us
    reduce_sum x2, other arithmetic, local(): tile_square = jnp.sum(query_f * query_f) + jnp.sum(keyval_f * keyval_f)  7.8 us
  transfers between devices with their start and end apart: 8, of which 4 were waited for; matrix products, arithmetic and copies ran while one was open for 12% of the time, Pallas kernels for 0%

profile of v1, /device:TPU:13, one launch (start us, length us, event | category | flops | bytes accessed | tf_op | source)
XLA Modules:
  0.0 362.5 jit_solution(15004594802166053011)
XLA Ops:
  7.2 0.0 all-gather.2.cloned.1.call-start
  7.2 2.1 pad_maximum_fusion.1
  9.3 0.0 all-gather.2.cloned.1.call-update
  9.3 0.0 reduce-scatter.2.cloned.1.call-start
  9.3 97.9 %all-gather.2.cloned.1.call-done = bf16[2048,1536]{1,0:T(8,128)(2,1)} async-done(((bf16[256,1536]{1,0:T(8,128)(2,1)}), bf16[2048,1536]{1,0:T(8,128)(2,1)}) %all-gather.2.cloned.1.call-update) | async-done | bytes 6291472 | tf_op jit(solution)/shard_map/all_gather | solution.py:22
  107.2 11.1 %convolution_convert_fusion = bf16[2048,1024]{1,0:T(8,128)(2,1)} fusion(bf16[2048,1536]{1,0:T(8,128)(2,1)} %all-gather.2.cloned.1.call-done, bf16[1024,512]{1,0:T(8,128)(2,1)} %param.12, bf16[1024,1024]{1,0:T(8,128)(2,1)} %param.11), kind=kOutput, calls=%fused_computation.6 | convolution fusion | flops 6450839552 | bytes 13631488 | tf_op jit(solution)/shard_map/dot_general | solution.py:24
  118.4 0.0 reduce-scatter.2.cloned.1.call-update
  118.4 0.0 copy-start
  118.4 3.3 multiply_reduce_fusion
  121.7 0.2 copy-done
  121.9 3.2 multiply_convert_fusion.1
  125.1 6.7 %copy.12 = bf16[256,8192]{0,1:T(8,128)(2,1)} copy(bf16[256,8192]{1,0:T(8,128)(2,1)} %multiply_convert_fusion.1) | data formatting | bytes 8388608 | tf_op jit(solution)/shard_map/convert_element_type | solution.py:13
  131.8 6.6 %all-to-all-start = ((bf16[256,8,1024]{0,2,1:T(8,128)(2,1)}), bf16[256,8,1024]{0,2,1:T(8,128)(2,1)}, u32[]{:S(2)}, u32[]{:S(2)}) async-start(bf16[256,8,1024]{0,2,1:T(8,128)(2,1)} %bitcast.18), calls=%async_computation.1 | async-start | bytes 8388608 | tf_op jit(solution)/shard_map/all_to_all | solution.py:64
  138.3 26.1 %reduce-scatter.2.cloned.1.call-done = bf16[512,1024]{1,0:T(8,128)(2,1)} async-done(((bf16[2048,1024]{1,0:T(8,128)(2,1)}), bf16[512,1024]{1,0:T(8,128)(2,1)}) %reduce-scatter.2.cloned.1.call-update) | async-done | bytes 1048592 | tf_op jit(solution)/shard_map/reduce_scatter | solution.py:27
  164.5 1.3 dynamic-slice_bitcast_fusion
  165.7 0.3 collective-permute-start.1
  166.1 0.9 collective-permute-start
  167.0 6.5 %convert_element_type.33 = f32[256,8192]{1,0:T(8,128)} convert(bf16[256,8192]{1,0:T(8,128)(2,1)} %param.7) | non-fusion elementwise | flops 2097152 | bytes 12582912 | tf_op jit(solution)/shard_map/convert_element_type | solution.py:11
  173.5 6.0 %collective-permute-done.1 = bf16[256,1024]{1,0:T(8,128)(2,1)S(1)} collective-permute-done((bf16[256,1024]{1,0:T(8,128)(2,1)S(1)}, bf16[256,1024]{1,0:T(8,128)(2,1)S(1)}, u32[]{:S(2)}, u32[]{:S(2)}) %collective-permute-start.1) | collective-permute-done | bytes 524320 | tf_op jit(solution)/shard_map/ppermute | solution.py:42
  179.5 0.4 fusion.16
  179.9 2.2 fusion.12
  182.1 0.1 collective-permute-start.2
  182.2 51.9 %all-to-all-done = bf16[256,8,1024]{0,2,1:T(8,128)(2,1)} async-done(((bf16[256,8,1024]{0,2,1:T(8,128)(2,1)}), bf16[256,8,1024]{0,2,1:T(8,128)(2,1)}, u32[]{:S(2)}, u32[]{:S(2)}) %all-to-all-start) | async-done | bytes 4194336 | tf_op jit(solution)/shard_map/all_to_all | solution.py:64
  234.1 12.6 %fusion = bf16[1024,1536]{1,0:T(8,128)(2,1)} fusion(bf16[8,256,1536]{2,1,0:T(8,128)(2,1)} %bitcast.22, bf16[256,8,1024]{0,2,1:T(8,128)(2,1)} %all-to-all-done), kind=kOutput, calls=%fused_computation.3 | convolution fusion | flops 6478626816 | bytes 13631488 | tf_op jit(solution)/shard_map/dot_general | solution.py:69
  246.7 19.6 %collective-permute-start.3 = (f32[2048]{0:T(1024)S(1)}, f32[2048]{0:T(1024)S(1)}, u32[]{:S(2)}, u32[]{:S(2)}) collective-permute-start(f32[2048]{0:T(1024)S(1)} %fusion.18), channel_id=1, source_target_pairs={{0,8},{4,12},{8,0},{12,4},{16,24},{20,28},{24,16},{28,20},{1,9},{5... | collective-permute-start | bytes 24584 | tf_op jit(solution)/shard_map/ppermute | solution.py:85
  266.3 4.5 %multiply_reduce_fusion.1 = (f32[]{:T(128)}, bf16[1024,1024]{1,0:T(8,128)(2,1)}) fusion(bf16[1024,1536]{1,0:T(8,128)(2,1)} %fusion), kind=kLoop, calls=%fused_computation.5 | loop fusion | flops 3145727 | bytes 4194308 | tf_op jit(solution)/shard_map/reduce_sum | solution.py:82
  270.9 28.1 %collective-permute-start.4 = (f32[2048]{0:T(1024)S(1)}, f32[2048]{0:T(1024)S(1)}, u32[]{:S(2)}, u32[]{:S(2)}) collective-permute-start(f32[2048]{0:T(1024)S(1)} %add.87), channel_id=1, source_target_pairs={{0,16},{4,20},{8,24},{12,28},{16,0},{20,4},{24,8},{28,12},{1,17},{... | collective-permute-start | bytes 24584 | tf_op jit(solution)/shard_map/ppermute | solution.py:85
  299.0 3.3 multiply_reduce_fusion.2
  303.6 5.1 %psum.14 = f32[256]{0:T(256)S(1)} all-reduce(f32[256]{0:T(256)S(1)} %get-tuple-element.6), channel_id=1, replica_groups=mesh['row'=8,'col'=4] {'col'}, use_global_device_ids=true, to_apply=%region_3.4 | all-reduce | flops 256 | bytes 2048 | tf_op jit(solution)/shard_map/psum | solution.py:56
  308.7 1.2 multiply_reduce_fusion.3
  310.6 3.3 fusion.9
  313.8 40.0 %psum.15 = f32[]{:T(128)} all-reduce(f32[]{:T(128)S(6)} %add.90), channel_id=1, replica_groups=mesh['row'=8,'col'=4] {'row','col'}, use_global_device_ids=true, to_apply=%region_9.10 | all-reduce | flops 1 | bytes 8 | tf_op jit(solution)/shard_map/psum | solution.py:91
  (13 shorter events, 0.0 us)
Async XLA Ops:
  7.2 100.1 %all-gather.2.cloned.1.call-start = ((), (), s32[]{:S(2)}) async-start(), calls=%async_computation.2 | async-start | bytes 7077888 | tf_op jit(solution)/shard_map/all_gather | solution.py:22
  9.3 155.2 %reduce-scatter.2.cloned.1.call-start = ((), (), s32[]{:S(2)}) async-start(), calls=%async_computation.3 | async-start | bytes 5242880 | tf_op jit(solution)/shard_map/reduce_scatter | solution.py:27
  118.4 3.3 copy-start.2
  118.4 3.5 copy-start
  131.8 102.3 %all-to-all-start = ((bf16[256,8,1024]{0,2,1:T(8,128)(2,1)}), bf16[256,8,1024]{0,2,1:T(8,128)(2,1)}, u32[]{:S(2)}, u32[]{:S(2)}) async-start(bf16[256,8,1024]{0,2,1:T(8,128)(2,1)} %bitcast.18), calls=%async_computation.1 | async-start | bytes 8388608 | tf_op jit(solution)/shard_map/all_to_all | solution.py:64
  165.7 13.7 %collective-permute-start.1 = (bf16[256,1024]{1,0:T(8,128)(2,1)S(1)}, bf16[256,1024]{1,0:T(8,128)(2,1)S(1)}, u32[]{:S(2)}, u32[]{:S(2)}) collective-permute-start(bf16[256,1024]{1,0:T(8,128)(2,1)S(1)} %get-tuple-element.15), channel_id=1, source_target_pairs={{0,4},{1,12},{2,20},{3,28},{4,0},{5,8},{6,16},{7,24},{8,5},{9,13},... | collective-permute-start | bytes 1572872 | tf_op jit(solution)/shard_map/ppermute | solution.py:42
  166.1 13.4 %collective-permute-start = (bf16[256,1024]{1,0:T(8,128)(2,1)S(1)}, bf16[256,1024]{1,0:T(8,128)(2,1)S(1)}, u32[]{:S(2)}, u32[]{:S(2)}) collective-permute-start(bf16[256,1024]{1,0:T(8,128)(2,1)S(1)} %get-tuple-element.16), channel_id=1, source_target_pairs={{0,0},{1,8},{2,16},{3,24},{4,4},{5,12},{6,20},{7,28},{8,1},{9,9},{... | collective-permute-start | bytes 1572872 | tf_op jit(solution)/shard_map/ppermute | solution.py:42
  182.1 64.6 %collective-permute-start.2 = (f32[2048]{0:T(1024)S(1)}, f32[2048]{0:T(1024)S(1)}, u32[]{:S(2)}, u32[]{:S(2)}) collective-permute-start(f32[2048]{0:T(1024)S(1)} %broadcast_multiply_fusion), channel_id=1, source_target_pairs={{0,4},{4,0},{8,12},{12,8},{16,20},{20,16},{24,28},{28,24},{1,5},{5... | collective-permute-start | bytes 24584 | tf_op jit(solution)/shard_map/ppermute | solution.py:85
  246.7 63.8 %copy-start.1 = (bf16[256,2048]{1,0:T(8,128)(2,1)S(1)}, bf16[256,2048]{1,0:T(8,128)(2,1)}, u32[]{:S(2)}) copy-start(bf16[256,2048]{1,0:T(8,128)(2,1)} %param.13) | copy-start | bytes 3145732
  246.7 24.2 %collective-permute-start.3 = (f32[2048]{0:T(1024)S(1)}, f32[2048]{0:T(1024)S(1)}, u32[]{:S(2)}, u32[]{:S(2)}) collective-permute-start(f32[2048]{0:T(1024)S(1)} %fusion.18), channel_id=1, source_target_pairs={{0,8},{4,12},{8,0},{12,4},{16,24},{20,28},{24,16},{28,20},{1,9},{5... | collective-permute-start | bytes 24584 | tf_op jit(solution)/shard_map/ppermute | solution.py:85
  270.9 37.8 %collective-permute-start.4 = (f32[2048]{0:T(1024)S(1)}, f32[2048]{0:T(1024)S(1)}, u32[]{:S(2)}, u32[]{:S(2)}) collective-permute-start(f32[2048]{0:T(1024)S(1)} %add.87), channel_id=1, source_target_pairs={{0,16},{4,20},{8,24},{12,28},{16,0},{20,4},{24,8},{28,12},{1,17},{... | collective-permute-start | bytes 24584 | tf_op jit(solution)/shard_map/ppermute | solution.py:85
Sparse Core Ops, SparseCore 0:
  10.7 96.4 all-gather.1
  118.5 45.9 reduce-scatter.1
